TPU v7x, 512 devices: a whole 4x8x8 slice. The times are simulated.
512 devices in a mesh: tp: 16 (over z, core), ep: 32 (over y, x).
Axes of the slice: x: 4, y: 8, z: 8, core: 2. Of those that a mesh axis runs over, the one named last changes fastest.
Arguments:
- tokens: bfloat16 [12288, 2048], P('ep', 'tp'), may hold values from -6 to 6
- norm_gain: float32 [2048], replicated, may hold values from 0.25 to 1.75
- shared_gate: bfloat16 [2048, 2816], P('ep', 'tp'), may hold values from -0.125 to 0.125
- shared_up: bfloat16 [2048, 2816], P('ep', 'tp'), may hold values from -0.125 to 0.125
- shared_down: bfloat16 [2816, 2048], P('tp', 'ep'), may hold values from -0.21875 to 0.21875
- expert_gate: bfloat16 [16, 32, 176, 2048], P('tp', 'ep'), may hold values from -0.125 to 0.125
- expert_up: bfloat16 [16, 32, 176, 2048], P('tp', 'ep'), may hold values from -0.125 to 0.125
- expert_down: bfloat16 [64, 1408, 2048], P('ep', None, 'tp'), may hold values from -0.15625 to 0.15625
- chosen: int32 [64, 384], P('ep'), may hold values from 0 to 12287, as said below
- gates: float32 [64, 384], P('ep'), may hold values from 0.1 to 1
Outputs:
- mixed: bfloat16 [12288, 2048], P('ep', 'tp')
Inputs may be any that keep to these rules, and one draw needn't show every extreme that they name: Each row of chosen holds 384 different token indices in rising order. Of one row, at most 24 lie among the 384 tokens of one index of ep (tokens s * 384 to (s + 1) * 384 - 1), and in every row exactly 24 lie among those of some index.
All inputs are finite; a program needn't handle non-finite values.
Results may differ from a plain program's by a relative error of at most 0.012.
Values may be sent and summed in bfloat16 or wider, within the bound.
A program may use at most 64 MiB of HBM per device.

v0:
```python
import jax
import jax.numpy as jnp
from jax import lax
from jax.sharding import PartitionSpec as P

EXP_DEV = 2
TOK_DEV = 384
CAP = 384
norm_eps = 1e-06


def side_by_side(arrays, axis, dim, along):
    both = jnp.concatenate(arrays, axis=along)
    whole, at, gathered = (lax.all_gather(both, axis, axis=dim, tiled=True), 0, [])
    for a in arrays:
        gathered.append(lax.slice_in_dim(whole, at, at + a.shape[along], axis=along))
        at += a.shape[along]
    return tuple(gathered)


def sent_to_all(array, axis):
    length = lax.axis_size(axis)
    return lax.all_to_all(
        jnp.broadcast_to(array[None], (length, *array.shape)), axis, 0, 0, tiled=True
    )


def joined_along(pieces, dim):
    dims = list(pieces.shape[1:])
    dims[dim] *= pieces.shape[0]
    return jnp.moveaxis(pieces, 0, dim).reshape(dims)


def gathered_copies(array, axis, dim):
    pieces = sent_to_all(array, axis)
    return joined_along(pieces, dim)


def on_device(
    tokens,
    norm_gain,
    shared_gate,
    shared_up,
    shared_down,
    expert_gate,
    expert_up,
    expert_down,
    chosen,
    gates,
):
    tp_count = lax.axis_size("tp")
    ep_count = lax.axis_size("ep")
    slice_width = tokens.shape[1]
    whole = lax.all_gather(tokens, "tp", axis=1, tiled=True)
    widened = whole.astype(jnp.float32)
    inv_scale = lax.rsqrt(jnp.mean(widened * widened, axis=1, keepdims=True) + norm_eps)
    normed = (widened * inv_scale * norm_gain).astype(jnp.bfloat16)
    pieces = side_by_side((shared_gate, shared_up), "ep", 0, 1)
    gate_sum = jnp.dot(normed, pieces[0], preferred_element_type=jnp.float32)
    up_sum = jnp.dot(normed, pieces[1], preferred_element_type=jnp.float32)
    shared_hidden = (jax.nn.silu(gate_sum) * up_sum).astype(jnp.bfloat16)
    partial_out = jnp.dot(
        shared_hidden, gathered_copies(shared_down, "ep", 1), preferred_element_type=jnp.float32
    )
    shared_part = lax.psum_scatter(
        partial_out.astype(jnp.bfloat16), "tp", scatter_dimension=1, tiled=True
    ).astype(jnp.float32)
    slot_most = 2 * CAP // ep_count
    slot_count = ep_count * slot_most
    sources = chosen // TOK_DEV
    source_flags = (
        sources[:, :, None] == jnp.arange(ep_count, dtype=jnp.int32)[None, None, :]
    ).astype(jnp.int32)
    counts = jnp.sum(source_flags, axis=1)
    starts = jnp.cumsum(counts, axis=1) - counts
    run_start = jnp.take_along_axis(starts, sources, axis=1)
    slot_index = sources * slot_most + jnp.arange(CAP, dtype=jnp.int32)[None, :] - run_start
    local_ids = chosen - sources * TOK_DEV
    expert_rows = jnp.arange(EXP_DEV, dtype=jnp.int32)[:, None]
    requests = (
        jnp.full((EXP_DEV, slot_count), TOK_DEV, jnp.int32)
        .at[expert_rows, slot_index]
        .set(local_ids)
    )
    requests = requests.reshape(EXP_DEV, ep_count, slot_most)
    asked_ids = lax.all_to_all(requests, "ep", split_axis=1, concat_axis=1, tiled=True)
    clipped = jnp.minimum(asked_ids, TOK_DEV - 1)
    local_expert = lax.axis_index("tp") // (tp_count // EXP_DEV)
    own_requests = lax.dynamic_index_in_dim(clipped, local_expert, 0, keepdims=False)
    outgoing = jnp.take(normed, own_requests.reshape(-1), axis=0).reshape(ep_count, slot_most, -1)
    arrived = lax.all_to_all(outgoing, "ep", split_axis=0, concat_axis=0, tiled=True)
    token_rows = arrived.reshape(slot_count, -1)
    gate_weight = expert_gate.reshape(expert_gate.shape[2], expert_gate.shape[3])
    up_weight = expert_up.reshape(expert_up.shape[2], expert_up.shape[3])
    gate_values = jnp.einsum(
        "hd,rd->hr", gate_weight, token_rows, preferred_element_type=jnp.float32
    )
    up_values = jnp.einsum("hd,rd->hr", up_weight, token_rows, preferred_element_type=jnp.float32)
    part_hidden = (jax.nn.silu(gate_values) * up_values).astype(jnp.bfloat16)
    all_hidden = lax.all_gather(part_hidden, "tp", axis=0, tiled=True)
    width_hidden = expert_down.shape[1]
    placed_rows = []
    for expert_slot in range(EXP_DEV):
        hidden_block = all_hidden[expert_slot * width_hidden : (expert_slot + 1) * width_hidden, :]
        outputs = jnp.einsum(
            "fr,fd->rd", hidden_block, expert_down[expert_slot], preferred_element_type=jnp.float32
        )
        gate_slots = (
            jnp.zeros((slot_count,), jnp.float32)
            .at[slot_index[expert_slot]]
            .set(gates[expert_slot])
        )
        placed = (gate_slots[:, None] * outputs).astype(jnp.bfloat16)
        placed_rows.append(placed)
    stacked = jnp.stack(placed_rows).reshape(EXP_DEV, ep_count, slot_most, slice_width)
    returned = lax.all_to_all(stacked, "ep", split_axis=1, concat_axis=1, tiled=True)
    flat_values = returned.reshape(-1, slice_width)
    flat_ids = asked_ids.reshape(-1)
    picker = (jnp.arange(TOK_DEV, dtype=jnp.int32)[:, None] == flat_ids[None, :]).astype(
        jnp.bfloat16
    )
    routed = jnp.dot(picker, flat_values, preferred_element_type=jnp.float32)
    return (shared_part + routed).astype(jnp.bfloat16)


def solution(mesh):
    return jax.shard_map(
        on_device,
        mesh=mesh,
        in_specs=(
            P("ep", "tp"),
            P(),
            P("ep", "tp"),
            P("ep", "tp"),
            P("tp", "ep"),
            P("tp", "ep", None, None),
            P("tp", "ep", None, None),
            P("ep", None, "tp"),
            P("ep", None),
            P("ep", None),
        ),
        out_specs=P("ep", "tp"),
        check_vma=False,
    )
```

profile of v0, /device:TPU:4, one launch (start us, length us, event | category | flops | bytes accessed | tf_op | source)
XLA Modules:
  0.0 284.9 jit_solution(4781293270764742484)
XLA Ops:
  7.4 0.7 all-gather.4.cloned.1.call-update
  8.1 0.7 multiply_subtract_fusion
  9.2 6.6 %gather_fusion.1 = s32[768]{0:T(1024)S(1)} fusion(s32[2,32]{1,0:T(2,128)S(1)} %sub.20, s32[768]{0:T(1024)S(1)} %reshape.168), kind=kCustom, calls=%fused_computation.1 | custom fusion | bytes 12288 | tf_op jit(solution)/shard_map/jit(take_along_axis)/gather | solution.py:76
  15.9 36.5 %scatter_fusion = s32[2,768]{1,0:T(2,128)S(1)} fusion(s32[2,768]{1,0:T(2,128)S(1)} %broadcast_in_dim.23, s32[768]{0:T(1024)S(1)} %reshape.174, s32[768]{0:T(1024)S(1)} %reshape.176), kind=kCustom, calls=%fused_computation.2 | custom fusion | bytes 15360 | tf_op jit(solution)/shard_map/scatter | solution.py:83
  53.1 10.2 %all-to-all-start.1 = ((s32[2,32,24]{2,0,1:T(2,128)}), s32[2,32,24]{2,0,1:T(2,128)S(1)}, u32[]{:S(2)}, u32[]{:S(2)}) async-start(s32[2,32,24]{2,0,1:T(2,128)} %copy.21), calls=%async_computation.1 | async-start | bytes 65536 | tf_op jit(solution)/shard_map/all_to_all | solution.py:86
  63.3 7.8 %all-to-all-done.1 = s32[2,32,24]{2,0,1:T(2,128)S(1)} async-done(((s32[2,32,24]{2,0,1:T(2,128)}), s32[2,32,24]{2,0,1:T(2,128)S(1)}, u32[]{:S(2)}, u32[]{:S(2)}) %all-to-all-start.1) | async-done | bytes 6176 | tf_op jit(solution)/shard_map/all_to_all | solution.py:86
  71.7 0.7 fusion.55
  72.6 1.9 fusion
  74.9 4.3 %gather_fusion = bf16[768,2048]{1,0:T(8,128)(2,1)} fusion(bf16[384,2048]{1,0:T(8,128)(2,1)S(1)} %fusion.2, s32[1024]{0:T(1024)S(1)} %pad_clamp_fusion), kind=kCustom, calls=%fused_computation | custom fusion | bytes 6294528 | tf_op jit(solution)/shard_map/jit(_take)/gather | solution.py:90
  79.2 3.9 %broadcast_select_fusion = bf16[32,24,2048]{2,1,0:T(8,128)(2,1)} fusion(bf16[32,24,2048]{2,1,0:T(8,128)(2,1)} %bitcast.63, pred[32,24]{1,0:T(8,128)(4,1)S(1)} %compare_and_fusion), kind=kLoop, calls=%fused_computation.10 | loop fusion | flops 1572864 | bytes 6292224 | tf_op jit(solution)/shard_map/jit(_take)/select_n | solution.py:90
  83.1 6.8 %all-to-all-start.2 = ((bf16[32,24,2048]{2,1,0:T(8,128)(2,1)}), bf16[32,24,2048]{2,1,0:T(8,128)(2,1)}, u32[]{:S(2)}, u32[]{:S(2)}) async-start(bf16[32,24,2048]{2,1,0:T(8,128)(2,1)} %broadcast_select_fusion), calls=%async_computation.2 | async-start | bytes 6291456 | tf_op jit(solution)/shard_map/all_to_all | solution.py:91
  90.0 0.7 pad_maximum_fusion.1
  90.8 73.0 %all-to-all-done.2 = bf16[32,24,2048]{2,1,0:T(8,128)(2,1)} async-done(((bf16[32,24,2048]{2,1,0:T(8,128)(2,1)}), bf16[32,24,2048]{2,1,0:T(8,128)(2,1)}, u32[]{:S(2)}, u32[]{:S(2)}) %all-to-all-start.2) | async-done | bytes 3145760 | tf_op jit(solution)/shard_map/all_to_all | solution.py:91
  163.8 3.2 %convolution_bitcast_fusion.1 = f32[176,768]{1,0:T(8,128)S(1)} fusion(bf16[768,2048]{1,0:T(8,128)(2,1)} %bitcast.7, bf16[1,1,176,2048]{3,2,1,0:T(8,128)(2,1)S(1)} %copy-done), kind=kOutput, calls=%fused_computation.19 | convolution fusion | flops 553648128 | bytes 4407296 | tf_op jit(solution)/shard_map/hd,rd->hr/dot_general | solution.py:95
  167.0 3.8 %fusion.9 = bf16[176,768]{1,0:T(8,128)(2,1)} fusion(bf16[768,2048]{1,0:T(8,128)(2,1)} %bitcast.7, bf16[1,1,176,2048]{3,2,1,0:T(8,128)(2,1)S(1)} %copy-done.8, f32[176,768]{1,0:T(8,128)S(1)} %convolution_bitcast_fusion.1), kind=kOutput, calls=%fused_computation.21 | convolution fusion | flops 554459136 | bytes 4677632 | tf_op jit(solution)/shard_map/hd,rd->hr/dot_general | solution.py:98
  170.9 1.1 broadcast_in_dim.19
  172.0 5.5 %all-to-all-start = ((bf16[32,176,64]{1,2,0:T(8,128)(2,1)}), bf16[32,176,64]{1,2,0:T(8,128)(2,1)S(1)}, u32[]{:S(2)}, u32[]{:S(2)}) async-start(bf16[32,176,64]{1,2,0:T(8,128)(2,1)} %broadcast_in_dim.19), calls=%async_computation | async-start | bytes 2097152 | tf_op jit(solution)/shard_map/all_to_all | solution.py:23
  177.5 9.4 %all-gather.6.cloned.1.call-done = bf16[2048,352]{1,0:T(8,128)(2,1)} async-done(((bf16[64,352]{1,0:T(8,128)(2,1)}), bf16[2048,352]{1,0:T(8,128)(2,1)}) %all-gather.6.cloned.1.call-update) | async-done | bytes 1441808 | tf_op jit(solution)/shard_map/all_gather | solution.py:14
  186.9 2.6 fusion.28
  189.5 14.7 %all-to-all-done = bf16[32,176,64]{1,2,0:T(8,128)(2,1)S(1)} async-done(((bf16[32,176,64]{1,2,0:T(8,128)(2,1)}), bf16[32,176,64]{1,2,0:T(8,128)(2,1)S(1)}, u32[]{:S(2)}, u32[]{:S(2)}) %all-to-all-start) | async-done | bytes 720928 | tf_op jit(solution)/shard_map/all_to_all | solution.py:23
  204.2 4.3 %convolution_convert_fusion = bf16[384,2048]{1,0:T(8,128)(2,1)} fusion(bf16[176,2048]{0,1:T(8,128)(2,1)S(1)} %bitcast.65, bf16[384,2048]{1,0:T(8,128)(2,1)S(1)} %fusion.2, bf16[2048,352]{1,0:T(8,128)(2,1)} %all-gather.6.cloned.1.call-done, f32[384,176]{0,1:T(8,128)} %fusion.28), kind=kOutput, calls=%fused_computation.11 | convolution fusion | flops 554840064 | bytes 5185536 | tf_op jit(solution)/shard_map/dot_general | solution.py:62
  208.5 2.7 copy.26
  211.3 3.1 %scatter_custom_fusion.1 = f32[768]{0:T(1024)S(1)} fusion(s32[384]{0:T(512)S(1)} %get-tuple-element.7, f32[384]{0:T(512)S(1)} %get-tuple-element.5, f32[]{:T(128)} %constant.48.clone.1), kind=kCustom, calls=%fused_computation.73 | custom fusion | bytes 3076 | tf_op jit(solution)/shard_map/scatter | solution.py:111
  214.4 2.9 %scatter_custom_fusion.2 = f32[768]{0:T(1024)S(1)} fusion(s32[384]{0:T(512)S(1)} %get-tuple-element.8, f32[384]{0:T(512)S(1)} %get-tuple-element.6, f32[]{:T(128)} %constant.48.clone.1), kind=kCustom, calls=%fused_computation.71 | custom fusion | bytes 3076 | tf_op jit(solution)/shard_map/scatter | solution.py:111
  217.3 16.4 %all-gather.8.cloned.1.call-done = bf16[2816,768]{1,0:T(8,128)(2,1)} async-done(((bf16[176,768]{1,0:T(8,128)(2,1)}), bf16[2816,768]{1,0:T(8,128)(2,1)}) %all-gather.8.cloned.1.call-update) | async-done | bytes 4325392 | tf_op jit(solution)/shard_map/all_gather | solution.py:100
  233.8 2.5 fusion.17
  236.7 0.8 fusion.20
  237.4 0.8 pad_maximum_fusion
  238.2 9.9 %all-to-all-start.3 = ((bf16[2,32,24,128]{3,2,0,1:T(8,128)(2,1)}), bf16[2,32,24,128]{3,2,0,1:T(8,128)(2,1)S(1)}, u32[]{:S(2)}, u32[]{:S(2)}) async-start(bf16[2,32,24,128]{3,2,0,1:T(8,128)(2,1)} %pad_maximum_fusion), calls=%async_computation.3 | async-start | bytes 786432 | tf_op jit(solution)/shard_map/all_to_all | solution.py:116
  248.2 27.1 %reduce-scatter.4.cloned.1.call-done = bf16[128,384]{1,0:T(8,128)(2,1)} async-done(((bf16[2048,384]{1,0:T(8,128)(2,1)}), bf16[128,384]{1,0:T(8,128)(2,1)}) %reduce-scatter.4.cloned.1.call-update) | async-done | bytes 98320
  275.3 1.0 copy.27
  276.3 1.2 fusion.25
  (53 shorter events, 2.9 us)
Async XLA Ops:
  7.4 156.5 %copy-start = (bf16[1,1,176,2048]{3,2,1,0:T(8,128)(2,1)S(1)}, bf16[1,1,176,2048]{3,2,1,0:T(8,128)(2,1)}, u32[]{:S(2)}) copy-start(bf16[1,1,176,2048]{3,2,1,0:T(8,128)(2,1)} %param.15) | copy-start | bytes 2162692
  7.4 65.2 %all-gather.4.cloned.1.call-start = ((), (), s32[]{:S(2)}) async-start(), calls=%async_computation.5 | async-start | bytes 1671168 | tf_op jit(solution)/shard_map/all_gather | solution.py:54
  15.8 58.6 %copy-start.5 = (f32[2048]{0:T(1024)S(1)}, f32[2048]{0:T(1024)}, u32[]{:S(2)}) copy-start(f32[2048]{0:T(1024)} %param.11) | copy-start | bytes 24580
  53.1 18.1 %all-to-all-start.1 = ((s32[2,32,24]{2,0,1:T(2,128)}), s32[2,32,24]{2,0,1:T(2,128)S(1)}, u32[]{:S(2)}, u32[]{:S(2)}) async-start(s32[2,32,24]{2,0,1:T(2,128)} %copy.21), calls=%async_computation.1 | async-start | bytes 65536 | tf_op jit(solution)/shard_map/all_to_all | solution.py:86
  72.6 1.9 copy-start.1
  83.1 6.9 %copy-start.2 = (bf16[64,176]{1,0:T(8,128)(2,1)S(1)}, bf16[64,176]{1,0:T(8,128)(2,1)}, u32[]{:S(2)}) copy-start(bf16[64,176]{1,0:T(8,128)(2,1)} %param.13) | copy-start | bytes 67588
  83.1 6.9 %copy-start.3 = (bf16[64,176]{1,0:T(8,128)(2,1)S(1)}, bf16[64,176]{1,0:T(8,128)(2,1)}, u32[]{:S(2)}) copy-start(bf16[64,176]{1,0:T(8,128)(2,1)} %param.12) | copy-start | bytes 67588
  83.1 80.7 %all-to-all-start.2 = ((bf16[32,24,2048]{2,1,0:T(8,128)(2,1)}), bf16[32,24,2048]{2,1,0:T(8,128)(2,1)}, u32[]{:S(2)}, u32[]{:S(2)}) async-start(bf16[32,24,2048]{2,1,0:T(8,128)(2,1)} %broadcast_select_fusion), calls=%async_computation.2 | async-start | bytes 6291456 | tf_op jit(solution)/shard_map/all_to_all | solution.py:91
  89.9 97.0 %all-gather.6.cloned.1.call-start = ((), (), s32[]{:S(2)}) async-start(), calls=%async_computation.6 | async-start | bytes 1622016 | tf_op jit(solution)/shard_map/all_gather | solution.py:14
  90.7 143.0 %all-gather.8.cloned.1.call-start = ((), (), s32[]{:S(2)}) async-start(), calls=%async_computation.7 | async-start | bytes 4595712 | tf_op jit(solution)/shard_map/all_gather | solution.py:100
  163.8 3.2 %copy-start.8 = (bf16[1,1,176,2048]{3,2,1,0:T(8,128)(2,1)S(1)}, bf16[1,1,176,2048]{3,2,1,0:T(8,128)(2,1)}, u32[]{:S(2)}) copy-start(bf16[1,1,176,2048]{3,2,1,0:T(8,128)(2,1)} %param.16) | copy-start | bytes 2162692
  167.0 3.8 %copy-start.4 = (bf16[176,64]{0,1:T(8,128)(2,1)S(1)}, bf16[176,64]{0,1:T(8,128)(2,1)}, u32[]{:S(2)}) copy-start(bf16[176,64]{0,1:T(8,128)(2,1)} %param.14) | copy-start | bytes 67588
  172.0 32.2 %all-to-all-start = ((bf16[32,176,64]{1,2,0:T(8,128)(2,1)}), bf16[32,176,64]{1,2,0:T(8,128)(2,1)S(1)}, u32[]{:S(2)}, u32[]{:S(2)}) async-start(bf16[32,176,64]{1,2,0:T(8,128)(2,1)} %broadcast_in_dim.19), calls=%async_computation | async-start | bytes 2097152 | tf_op jit(solution)/shard_map/all_to_all | solution.py:23
  177.5 97.8 %reduce-scatter.4.cloned.1.call-start = ((), (), s32[]{:S(2)}) async-start(), calls=%async_computation.8 | async-start | bytes 1671168
  208.5 2.7 copy-start.6
  208.5 25.3 %copy-start.9 = (bf16[2,1408,128]{2,1,0:T(8,128)(2,1)S(1)}, bf16[2,1408,128]{2,1,0:T(8,128)(2,1)}, u32[]{:S(2)}) copy-start(bf16[2,1408,128]{2,1,0:T(8,128)(2,1)} %param.17) | copy-start | bytes 2162692
  233.8 2.9 %copy-start.7 = (bf16[2816,768]{1,0:T(8,128)(2,1)S(1)}, bf16[2816,768]{1,0:T(8,128)(2,1)}, u32[]{:S(2)}) copy-start(bf16[2816,768]{1,0:T(8,128)(2,1)} %all-gather.8.cloned.1.call-done) | copy-start | bytes 12976132
  238.2 38.1 %all-to-all-start.3 = ((bf16[2,32,24,128]{3,2,0,1:T(8,128)(2,1)}), bf16[2,32,24,128]{3,2,0,1:T(8,128)(2,1)S(1)}, u32[]{:S(2)}, u32[]{:S(2)}) async-start(bf16[2,32,24,128]{3,2,0,1:T(8,128)(2,1)} %pad_maximum_fusion), calls=%async_computation.3 | async-start | bytes 786432 | tf_op jit(solution)/shard_map/all_to_all | solution.py:116
Sparse Core Ops, SparseCore 0:
  10.2 46.8 all-gather.3
  211.4 63.8 reduce-scatter.3
Sparse Core Ops, SparseCore 1:
  93.6 93.3 all-gather.5
  188.9 44.8 all-gather.7
where the time goes:
time: 286 us; the launch traced here: 285 us
  waiting for transfers between devices  149 us (52%)
  local copies, waits for them, and re-layouts  60.1 us (21%)
  starting transfers between devices  32.5 us (11%)
  matrix products  18.4 us (6%)
  between operations  15.2 us (5%)
  other arithmetic  9.57 us (3%)
    all_to_all x1, waiting for transfers between devices, on_device(): lax.all_to_all(outgoing, 'ep', split_axis=0, concat_axis=0, tiled=True)  73 us
    scatter x1, local copies, waits for them, and re-layouts, on_device(): requests = jnp.full((EXP_DEV, slot_count), TOK_DEV, jnp.int32).at[expert_...  36.5 us
    unnamed x5, waiting for transfers between devices  27.8 us
    all_gather x1, waiting for transfers between devices, on_device(): all_hidden = lax.all_gather(part_hidden, 'tp', axis=0, tiled=True)  16.4 us
    all_to_all x1, waiting for transfers between devices, sent_to_all(): lax.all_to_all(jnp.broadcast_to(array[None], (length, *array.shape)), axi...  14.7 us
    all_to_all x1, starting transfers between devices, on_device(): lax.all_to_all(requests, 'ep', split_axis=1, concat_axis=1, tiled=True)  10.2 us
    all_to_all x1, starting transfers between devices, on_device(): lax.all_to_all(stacked, 'ep', split_axis=1, concat_axis=1, tiled=True)  9.87 us
    all_gather x1, waiting for transfers between devices, side_by_side(): lax.all_gather(both, axis, axis=dim, tiled=True)  9.39 us
  transfers between devices with their start and end apart: 8, of which 6 were waited for; matrix products, arithmetic and copies ran while one was open for 27% of the time, Pallas kernels for 0%

commit v1 on v0

--- a/solution.py
+++ b/solution.py
@@ -97,7 +97,16 @@
     )
     up_values = jnp.einsum("hd,rd->hr", up_weight, token_rows, preferred_element_type=jnp.float32)
     part_hidden = (jax.nn.silu(gate_values) * up_values).astype(jnp.bfloat16)
-    all_hidden = lax.all_gather(part_hidden, "tp", axis=0, tiled=True)
+    ways = lax.axis_size("tp")
+    up = [(d, (d + 1) % ways) for d in range(ways)]
+    down = [(d, (d - 1) % ways) for d in range(ways)]
+    earlier, later = ([part_hidden], [part_hidden])
+    for _ in range(ways // 2):
+        earlier.append(lax.ppermute(earlier[-1], "tp", up))
+    for _ in range((ways - 1) // 2):
+        later.append(lax.ppermute(later[-1], "tp", down))
+    line = jnp.concatenate([*earlier[::-1], *later[1:]], axis=0)
+    all_hidden = jnp.roll(line, (lax.axis_index("tp") - ways // 2) * part_hidden.shape[0], axis=0)
     width_hidden = expert_down.shape[1]
     placed_rows = []
     for expert_slot in range(EXP_DEV):

time: 286 us -> 314 us (1.098)
  starting transfers between devices: 32.5 us -> 54 us
  local copies, waits for them, and re-layouts: 60.1 us -> 78.3 us
  waiting for transfers between devices: 149 us -> 137 us
    ppermute x0 -> x15, waiting for transfers between devices: none -> 26.5 us  [the longest x7 13.6 us: on_device(): later.append(lax.ppermute(later[-1], 'tp', down))]
    ppermute x0 -> x15, starting transfers between devices: none -> 21.8 us  [the longest x7 21.8 us: on_device(): later.append(lax.ppermute(later[-1], 'tp', down))]
    unnamed x22 -> x59, local copies, waits for them, and re-layouts: 4.1 us -> 22.2 us
    all_gather x1 -> x0, waiting for transfers between devices: 16.4 us -> none  [on_device(): all_hidden = lax.all_gather(part_hidden, 'tp', axis=0, tiled=True)]
    all_to_all x1, waiting for transfers between devices: 14.7 us -> 0.01 us  [sent_to_all(): lax.all_to_all(jnp.broadcast_to(array[None], (length, *array.shape)), axi...]
    all_gather x1, waiting for transfers between devices: 9.39 us -> 0.01 us  [side_by_side(): lax.all_gather(both, axis, axis=dim, tiled=True)]
    unnamed x5 -> x4, waiting for transfers between devices: 27.8 us -> 30 us
  transfers between devices with their start and end apart: 8 -> 22, of which waited for: 6 -> 8; matrix products, arithmetic and copies ran while one was open for 27% -> 29% of each run, Pallas kernels for 0% -> 0%
where the time goes in v1:
time: 314 us; the launch traced here: 312 us
  waiting for transfers between devices  137 us (44%)
  local copies, waits for them, and re-layouts  78.3 us (25%)
  starting transfers between devices  54 us (17%)
  matrix products  16.4 us (5%)
  between operations  15.4 us (5%)
  other arithmetic  10.8 us (3%)
    all_to_all x1, waiting for transfers between devices, on_device(): lax.all_to_all(outgoing, 'ep', split_axis=0, concat_axis=0, tiled=True)  73.1 us
    scatter x1, local copies, waits for them, and re-layouts, on_device(): requests = jnp.full((EXP_DEV, slot_count), TOK_DEV, jnp.int32).at[expert_...  36.5 us
    unnamed x4, waiting for transfers between devices  30 us
    unnamed x59, local copies, waits for them, and re-layouts  22.2 us
    ppermute x7, starting transfers between devices, on_device(): later.append(lax.ppermute(later[-1], 'tp', down))  21.8 us
    ppermute x7, waiting for transfers between devices, on_device(): later.append(lax.ppermute(later[-1], 'tp', down))  13.6 us
    ppermute x8, waiting for transfers between devices, on_device(): earlier.append(lax.ppermute(earlier[-1], 'tp', up))  12.9 us
    all_to_all x1, starting transfers between devices, on_device(): lax.all_to_all(requests, 'ep', split_axis=1, concat_axis=1, tiled=True)  10.2 us
  transfers between devices with their start and end apart: 22, of which 8 were waited for; matrix products, arithmetic and copies ran while one was open for 29% of the time, Pallas kernels for 0%

profile of v1, /device:TPU:4, one launch (start us, length us, event | category | flops | bytes accessed | tf_op | source)
XLA Modules:
  0.0 312.4 jit_solution(16419233760693024892)
XLA Ops:
  9.2 6.6 %gather_fusion.1 = s32[768]{0:T(1024)S(1)} fusion(s32[2,32]{1,0:T(2,128)S(1)} %sub.27, s32[768]{0:T(1024)S(1)} %reshape.168), kind=kCustom, calls=%fused_computation.1 | custom fusion | bytes 12288 | tf_op jit(solution)/shard_map/jit(take_along_axis)/gather | solution.py:76
  15.8 36.5 %scatter_fusion = s32[2,768]{1,0:T(2,128)S(1)} fusion(s32[2,768]{1,0:T(2,128)S(1)} %broadcast_in_dim.23, s32[768]{0:T(1024)S(1)} %reshape.174, s32[768]{0:T(1024)S(1)} %reshape.176), kind=kCustom, calls=%fused_computation.2 | custom fusion | bytes 15360 | tf_op jit(solution)/shard_map/scatter | solution.py:83
  53.1 10.2 %all-to-all-start.1 = ((s32[2,32,24]{2,0,1:T(2,128)}), s32[2,32,24]{2,0,1:T(2,128)S(1)}, u32[]{:S(2)}, u32[]{:S(2)}) async-start(s32[2,32,24]{2,0,1:T(2,128)} %copy.21), calls=%async_computation.1 | async-start | bytes 65536 | tf_op jit(solution)/shard_map/all_to_all | solution.py:86
  63.3 7.8 %all-to-all-done.1 = s32[2,32,24]{2,0,1:T(2,128)S(1)} async-done(((s32[2,32,24]{2,0,1:T(2,128)}), s32[2,32,24]{2,0,1:T(2,128)S(1)}, u32[]{:S(2)}, u32[]{:S(2)}) %all-to-all-start.1) | async-done | bytes 6176 | tf_op jit(solution)/shard_map/all_to_all | solution.py:86
  72.6 1.8 fusion
  74.4 1.8 fusion.2
  76.2 4.3 %gather_fusion = bf16[768,2048]{1,0:T(8,128)(2,1)} fusion(bf16[384,2048]{1,0:T(8,128)(2,1)S(1)} %fusion.2, s32[1024]{0:T(1024)S(1)} %pad_clamp_fusion), kind=kCustom, calls=%fused_computation | custom fusion | bytes 6294528 | tf_op jit(solution)/shard_map/jit(_take)/gather | solution.py:90
  80.5 3.9 %broadcast_select_fusion = bf16[32,24,2048]{2,1,0:T(8,128)(2,1)} fusion(bf16[32,24,2048]{2,1,0:T(8,128)(2,1)} %bitcast.63, pred[32,24]{1,0:T(8,128)(4,1)S(1)} %compare_and_fusion), kind=kLoop, calls=%fused_computation.10 | loop fusion | flops 1572864 | bytes 6292224 | tf_op jit(solution)/shard_map/jit(_take)/select_n | solution.py:90
  84.4 6.7 %all-to-all-start.2 = ((bf16[32,24,2048]{2,1,0:T(8,128)(2,1)}), bf16[32,24,2048]{2,1,0:T(8,128)(2,1)}, u32[]{:S(2)}, u32[]{:S(2)}) async-start(bf16[32,24,2048]{2,1,0:T(8,128)(2,1)} %broadcast_select_fusion), calls=%async_computation.2 | async-start | bytes 6291456 | tf_op jit(solution)/shard_map/all_to_all | solution.py:91
  91.8 73.1 %all-to-all-done.2 = bf16[32,24,2048]{2,1,0:T(8,128)(2,1)} async-done(((bf16[32,24,2048]{2,1,0:T(8,128)(2,1)}), bf16[32,24,2048]{2,1,0:T(8,128)(2,1)}, u32[]{:S(2)}, u32[]{:S(2)}) %all-to-all-start.2) | async-done | bytes 3145760 | tf_op jit(solution)/shard_map/all_to_all | solution.py:91
  165.0 3.1 convolution_bitcast_fusion.1
  168.1 3.3 %fusion.9 = bf16[176,768]{1,0:T(8,128)(2,1)S(1)} fusion(bf16[768,2048]{1,0:T(8,128)(2,1)} %bitcast.7, bf16[1,1,176,2048]{3,2,1,0:T(8,128)(2,1)} %param.16, f32[176,768]{1,0:T(8,128)S(1)} %convolution_bitcast_fusion.1), kind=kOutput, calls=%fused_computation.21 | convolution fusion | flops 554459136 | bytes 4677632 | tf_op jit(solution)/shard_map/hd,rd->hr/dot_general | solution.py:98
  171.4 12.9 %collective-permute-done = bf16[176,768]{1,0:T(8,128)(2,1)S(1)} collective-permute-done((bf16[176,768]{1,0:T(8,128)(2,1)S(1)}, bf16[176,768]{1,0:T(8,128)(2,1)S(1)}, u32[]{:S(2)}, u32[]{:S(2)}) %collective-permute-start) | collective-permute-done | bytes 270368 | tf_op jit(solution)/shard_map/ppermute | solution.py:105
  185.4 5.2 %all-to-all-start = ((bf16[32,176,64]{1,2,0:T(8,128)(2,1)}), bf16[32,176,64]{1,2,0:T(8,128)(2,1)}, u32[]{:S(2)}, u32[]{:S(2)}) async-start(bf16[32,176,64]{1,2,0:T(8,128)(2,1)} %broadcast_in_dim.19), calls=%async_computation | async-start | bytes 2097152 | tf_op jit(solution)/shard_map/all_to_all | solution.py:23
  190.7 2.4 collective-permute-start.8
  193.1 4.0 %collective-permute-done.8 = bf16[176,768]{1,0:T(8,128)(2,1)S(1)} collective-permute-done((bf16[176,768]{1,0:T(8,128)(2,1)S(1)}, bf16[176,768]{1,0:T(8,128)(2,1)S(1)}, u32[]{:S(2)}, u32[]{:S(2)}) %collective-permute-start.8) | collective-permute-done | bytes 270368 | tf_op jit(solution)/shard_map/ppermute | solution.py:107
  197.0 3.4 %collective-permute-start.9 = (bf16[176,768]{1,0:T(8,128)(2,1)S(1)}, bf16[176,768]{1,0:T(8,128)(2,1)S(1)}, u32[]{:S(2)}, u32[]{:S(2)}) collective-permute-start(bf16[176,768]{1,0:T(8,128)(2,1)S(1)} %collective-permute-done.8), channel_id=1, source_target_pairs={{0,480},{32,0},{64,32},{96,64},{128,96},{160,128},{192,160},{224,1... | collective-permute-start | bytes 811016 | tf_op jit(solution)/shard_map/ppermute | solution.py:107
  200.4 4.0 %collective-permute-done.9 = bf16[176,768]{1,0:T(8,128)(2,1)S(1)} collective-permute-done((bf16[176,768]{1,0:T(8,128)(2,1)S(1)}, bf16[176,768]{1,0:T(8,128)(2,1)S(1)}, u32[]{:S(2)}, u32[]{:S(2)}) %collective-permute-start.9) | collective-permute-done | bytes 270368 | tf_op jit(solution)/shard_map/ppermute | solution.py:107
  205.1 3.5 %collective-permute-start.10 = (bf16[176,768]{1,0:T(8,128)(2,1)S(1)}, bf16[176,768]{1,0:T(8,128)(2,1)}, u32[]{:S(2)}, u32[]{:S(2)}) collective-permute-start(bf16[176,768]{1,0:T(8,128)(2,1)S(1)} %collective-permute-done.9), channel_id=1, source_target_pairs={{0,480},{32,0},{64,32},{96,64},{128,96},{160,128},{192,160},{224,1... | collective-permute-start | bytes 811016 | tf_op jit(solution)/shard_map/ppermute | solution.py:107
  208.6 4.0 %collective-permute-done.10 = bf16[176,768]{1,0:T(8,128)(2,1)} collective-permute-done((bf16[176,768]{1,0:T(8,128)(2,1)S(1)}, bf16[176,768]{1,0:T(8,128)(2,1)}, u32[]{:S(2)}, u32[]{:S(2)}) %collective-permute-start.10) | collective-permute-done | bytes 270368 | tf_op jit(solution)/shard_map/ppermute | solution.py:107
  212.6 3.5 %collective-permute-start.11 = (bf16[176,768]{1,0:T(8,128)(2,1)}, bf16[176,768]{1,0:T(8,128)(2,1)}, u32[]{:S(2)}, u32[]{:S(2)}) collective-permute-start(bf16[176,768]{1,0:T(8,128)(2,1)} %collective-permute-done.10), channel_id=1, source_target_pairs={{0,480},{32,0},{64,32},{96,64},{128,96},{160,128},{192,160},{224,1... | collective-permute-start | bytes 811016 | tf_op jit(solution)/shard_map/ppermute | solution.py:107
  216.2 2.9 scatter_custom_fusion.1
  219.1 3.1 scatter_custom_fusion.2
  222.3 2.9 collective-permute-start.12
  225.2 2.6 fusion.28
  227.8 1.7 collective-permute-done.12
  229.5 3.1 collective-permute-start.13
  232.6 4.6 %convolution_convert_fusion = bf16[384,2048]{1,0:T(8,128)(2,1)} fusion(bf16[176,2048]{0,1:T(8,128)(2,1)} %bitcast.1, bf16[384,2048]{1,0:T(8,128)(2,1)S(1)} %fusion.2, bf16[2048,352]{1,0:T(8,128)(2,1)} %all-gather.5.cloned.1.call-done, f32[384,176]{0,1:T(8,128)} %fusion.28), kind=kOutput, calls=%fused_computation.11 | convolution fusion | flops 554840064 | bytes 5513216 | tf_op jit(solution)/shard_map/dot_general | solution.py:62
  237.3 2.7 copy.26
  240.0 3.0 collective-permute-start.14
  263.4 9.9 %all-to-all-start.3 = ((bf16[2,32,24,128]{3,2,0,1:T(8,128)(2,1)}), bf16[2,32,24,128]{3,2,0,1:T(8,128)(2,1)S(1)}, u32[]{:S(2)}, u32[]{:S(2)}) async-start(bf16[2,32,24,128]{3,2,0,1:T(8,128)(2,1)} %pad_maximum_fusion), calls=%async_computation.3 | async-start | bytes 786432 | tf_op jit(solution)/shard_map/all_to_all | solution.py:125
  273.4 29.3 %reduce-scatter.4.cloned.1.call-done = bf16[128,384]{1,0:T(8,128)(2,1)} async-done(((bf16[2048,384]{1,0:T(8,128)(2,1)}), bf16[128,384]{1,0:T(8,128)(2,1)}) %reduce-scatter.4.cloned.1.call-update) | async-done | bytes 98320
  (118 shorter events, 29.2 us)
Async XLA Ops:
  7.4 157.6 %copy-start = (bf16[1,1,176,2048]{3,2,1,0:T(8,128)(2,1)S(1)}, bf16[1,1,176,2048]{3,2,1,0:T(8,128)(2,1)}, u32[]{:S(2)}) copy-start(bf16[1,1,176,2048]{3,2,1,0:T(8,128)(2,1)} %param.15) | copy-start | bytes 2162692
  7.4 67.0 %copy-start.10 = (f32[2048]{0:T(1024)S(1)}, f32[2048]{0:T(1024)}, u32[]{:S(2)}) copy-start(f32[2048]{0:T(1024)} %param.11) | copy-start | bytes 24580
  7.4 65.2 %all-gather.3.cloned.1.call-start = ((), (), s32[]{:S(2)}) async-start(), calls=%async_computation.5 | async-start | bytes 1671168 | tf_op jit(solution)/shard_map/all_gather | solution.py:54
  53.1 18.1 %all-to-all-start.1 = ((s32[2,32,24]{2,0,1:T(2,128)}), s32[2,32,24]{2,0,1:T(2,128)S(1)}, u32[]{:S(2)}, u32[]{:S(2)}) async-start(s32[2,32,24]{2,0,1:T(2,128)} %copy.21), calls=%async_computation.1 | async-start | bytes 65536 | tf_op jit(solution)/shard_map/all_to_all | solution.py:86
  80.5 10.6 %copy-start.8 = (bf16[64,176]{1,0:T(8,128)(2,1)S(1)}, bf16[64,176]{1,0:T(8,128)(2,1)}, u32[]{:S(2)}) copy-start(bf16[64,176]{1,0:T(8,128)(2,1)} %param.12) | copy-start | bytes 67588
  84.4 80.6 %all-to-all-start.2 = ((bf16[32,24,2048]{2,1,0:T(8,128)(2,1)}), bf16[32,24,2048]{2,1,0:T(8,128)(2,1)}, u32[]{:S(2)}, u32[]{:S(2)}) async-start(bf16[32,24,2048]{2,1,0:T(8,128)(2,1)} %broadcast_select_fusion), calls=%async_computation.2 | async-start | bytes 6291456 | tf_op jit(solution)/shard_map/all_to_all | solution.py:91
  91.0 93.2 %copy-start.9 = (bf16[176,64]{0,1:T(8,128)(2,1)S(1)}, bf16[176,64]{0,1:T(8,128)(2,1)}, u32[]{:S(2)}) copy-start(bf16[176,64]{0,1:T(8,128)(2,1)} %param.14) | copy-start | bytes 67588
  91.0 134.2 %all-gather.5.cloned.1.call-start = ((), (), s32[]{:S(2)}) async-start(), calls=%async_computation.6 | async-start | bytes 1622016 | tf_op jit(solution)/shard_map/all_gather | solution.py:14
  164.9 51.2 %copy-start.11 = (f32[2,384]{1,0:T(2,128)S(1)}, f32[2,384]{1,0:T(2,128)}, u32[]{:S(2)}) copy-start(f32[2,384]{1,0:T(2,128)} %param.19) | copy-start | bytes 9220
  171.3 12.9 %collective-permute-start = (bf16[176,768]{1,0:T(8,128)(2,1)S(1)}, bf16[176,768]{1,0:T(8,128)(2,1)S(1)}, u32[]{:S(2)}, u32[]{:S(2)}) collective-permute-start(bf16[176,768]{1,0:T(8,128)(2,1)S(1)} %fusion.9), channel_id=1, source_target_pairs={{0,32},{32,64},{64,96},{96,128},{128,160},{160,192},{192,224},{224... | collective-permute-start | bytes 811016 | tf_op jit(solution)/shard_map/ppermute | solution.py:105
  184.3 8.8 %collective-permute-start.1 = (bf16[176,768]{1,0:T(8,128)(2,1)S(1)}, bf16[176,768]{1,0:T(8,128)(2,1)S(1)}, u32[]{:S(2)}, u32[]{:S(2)}) collective-permute-start(bf16[176,768]{1,0:T(8,128)(2,1)S(1)} %collective-permute-done), channel_id=1, source_target_pairs={{0,32},{32,64},{64,96},{96,128},{128,160},{160,192},{192,224},{224... | collective-permute-start | bytes 811016 | tf_op jit(solution)/shard_map/ppermute | solution.py:105
  185.4 47.2 %all-to-all-start = ((bf16[32,176,64]{1,2,0:T(8,128)(2,1)}), bf16[32,176,64]{1,2,0:T(8,128)(2,1)}, u32[]{:S(2)}, u32[]{:S(2)}) async-start(bf16[32,176,64]{1,2,0:T(8,128)(2,1)} %broadcast_in_dim.19), calls=%async_computation | async-start | bytes 2097152 | tf_op jit(solution)/shard_map/all_to_all | solution.py:23
  190.6 112.1 %reduce-scatter.4.cloned.1.call-start = ((), (), s32[]{:S(2)}) async-start(), calls=%async_computation.7 | async-start | bytes 1671168
  190.7 6.4 %collective-permute-start.8 = (bf16[176,768]{1,0:T(8,128)(2,1)S(1)}, bf16[176,768]{1,0:T(8,128)(2,1)S(1)}, u32[]{:S(2)}, u32[]{:S(2)}) collective-permute-start(bf16[176,768]{1,0:T(8,128)(2,1)S(1)} %fusion.9), channel_id=1, source_target_pairs={{0,480},{32,0},{64,32},{96,64},{128,96},{160,128},{192,160},{224,1... | collective-permute-start | bytes 811016 | tf_op jit(solution)/shard_map/ppermute | solution.py:107
  193.1 7.3 %collective-permute-start.2 = (bf16[176,768]{1,0:T(8,128)(2,1)S(1)}, bf16[176,768]{1,0:T(8,128)(2,1)S(1)}, u32[]{:S(2)}, u32[]{:S(2)}) collective-permute-start(bf16[176,768]{1,0:T(8,128)(2,1)S(1)} %collective-permute-done.1), channel_id=1, source_target_pairs={{0,32},{32,64},{64,96},{96,128},{128,160},{160,192},{192,224},{224... | collective-permute-start | bytes 811016 | tf_op jit(solution)/shard_map/ppermute | solution.py:105
  197.0 7.3 %collective-permute-start.9 = (bf16[176,768]{1,0:T(8,128)(2,1)S(1)}, bf16[176,768]{1,0:T(8,128)(2,1)S(1)}, u32[]{:S(2)}, u32[]{:S(2)}) collective-permute-start(bf16[176,768]{1,0:T(8,128)(2,1)S(1)} %collective-permute-done.8), channel_id=1, source_target_pairs={{0,480},{32,0},{64,32},{96,64},{128,96},{160,128},{192,160},{224,1... | collective-permute-start | bytes 811016 | tf_op jit(solution)/shard_map/ppermute | solution.py:107
  200.4 12.2 %copy-start.3 = (bf16[176,768]{1,0:T(8,128)(2,1)}, bf16[176,768]{1,0:T(8,128)(2,1)S(1)}, u32[]{:S(2)}) copy-start(bf16[176,768]{1,0:T(8,128)(2,1)S(1)} %collective-permute-done.2) | copy-start | bytes 811012
  200.4 8.2 %collective-permute-start.3 = (bf16[176,768]{1,0:T(8,128)(2,1)S(1)}, bf16[176,768]{1,0:T(8,128)(2,1)S(1)}, u32[]{:S(2)}, u32[]{:S(2)}) collective-permute-start(bf16[176,768]{1,0:T(8,128)(2,1)S(1)} %collective-permute-done.2), channel_id=1, source_target_pairs={{0,32},{32,64},{64,96},{96,128},{128,160},{160,192},{192,224},{224... | collective-permute-start | bytes 811016 | tf_op jit(solution)/shard_map/ppermute | solution.py:105
  205.1 7.5 %collective-permute-start.10 = (bf16[176,768]{1,0:T(8,128)(2,1)S(1)}, bf16[176,768]{1,0:T(8,128)(2,1)}, u32[]{:S(2)}, u32[]{:S(2)}) collective-permute-start(bf16[176,768]{1,0:T(8,128)(2,1)S(1)} %collective-permute-done.9), channel_id=1, source_target_pairs={{0,480},{32,0},{64,32},{96,64},{128,96},{160,128},{192,160},{224,1... | collective-permute-start | bytes 811016 | tf_op jit(solution)/shard_map/ppermute | solution.py:107
  208.6 7.5 %collective-permute-start.4 = (bf16[176,768]{1,0:T(8,128)(2,1)S(1)}, bf16[176,768]{1,0:T(8,128)(2,1)}, u32[]{:S(2)}, u32[]{:S(2)}) collective-permute-start(bf16[176,768]{1,0:T(8,128)(2,1)S(1)} %collective-permute-done.3), channel_id=1, source_target_pairs={{0,32},{32,64},{64,96},{96,128},{128,160},{160,192},{192,224},{224... | collective-permute-start | bytes 811016 | tf_op jit(solution)/shard_map/ppermute | solution.py:105
  212.6 9.7 %collective-permute-start.11 = (bf16[176,768]{1,0:T(8,128)(2,1)}, bf16[176,768]{1,0:T(8,128)(2,1)}, u32[]{:S(2)}, u32[]{:S(2)}) collective-permute-start(bf16[176,768]{1,0:T(8,128)(2,1)} %collective-permute-done.10), channel_id=1, source_target_pairs={{0,480},{32,0},{64,32},{96,64},{128,96},{160,128},{192,160},{224,1... | collective-permute-start | bytes 811016 | tf_op jit(solution)/shard_map/ppermute | solution.py:107
  216.1 9.1 %collective-permute-start.5 = (bf16[176,768]{1,0:T(8,128)(2,1)}, bf16[176,768]{1,0:T(8,128)(2,1)}, u32[]{:S(2)}, u32[]{:S(2)}) collective-permute-start(bf16[176,768]{1,0:T(8,128)(2,1)} %collective-permute-done.4), channel_id=1, source_target_pairs={{0,32},{32,64},{64,96},{96,128},{128,160},{160,192},{192,224},{224... | collective-permute-start | bytes 811016 | tf_op jit(solution)/shard_map/ppermute | solution.py:105
  222.3 7.2 %collective-permute-start.12 = (bf16[176,768]{1,0:T(8,128)(2,1)}, bf16[176,768]{1,0:T(8,128)(2,1)}, u32[]{:S(2)}, u32[]{:S(2)}) collective-permute-start(bf16[176,768]{1,0:T(8,128)(2,1)} %collective-permute-done.11), channel_id=1, source_target_pairs={{0,480},{32,0},{64,32},{96,64},{128,96},{160,128},{192,160},{224,1... | collective-permute-start | bytes 811016 | tf_op jit(solution)/shard_map/ppermute | solution.py:107
  225.2 7.4 %collective-permute-start.6 = (bf16[176,768]{1,0:T(8,128)(2,1)}, bf16[176,768]{1,0:T(8,128)(2,1)}, u32[]{:S(2)}, u32[]{:S(2)}) collective-permute-start(bf16[176,768]{1,0:T(8,128)(2,1)} %collective-permute-done.5), channel_id=1, source_target_pairs={{0,32},{32,64},{64,96},{96,128},{128,160},{160,192},{192,224},{224... | collective-permute-start | bytes 811016 | tf_op jit(solution)/shard_map/ppermute | solution.py:105
  229.5 10.5 %collective-permute-start.13 = (bf16[176,768]{1,0:T(8,128)(2,1)}, bf16[176,768]{1,0:T(8,128)(2,1)}, u32[]{:S(2)}, u32[]{:S(2)}) collective-permute-start(bf16[176,768]{1,0:T(8,128)(2,1)} %collective-permute-done.12), channel_id=1, source_target_pairs={{0,480},{32,0},{64,32},{96,64},{128,96},{160,128},{192,160},{224,1... | collective-permute-start | bytes 811016 | tf_op jit(solution)/shard_map/ppermute | solution.py:107
  232.6 10.4 %collective-permute-start.7 = (bf16[176,768]{1,0:T(8,128)(2,1)}, bf16[176,768]{1,0:T(8,128)(2,1)}, u32[]{:S(2)}, u32[]{:S(2)}) collective-permute-start(bf16[176,768]{1,0:T(8,128)(2,1)} %collective-permute-done.6), channel_id=1, source_target_pairs={{0,32},{32,64},{64,96},{96,128},{128,160},{160,192},{192,224},{224... | collective-permute-start | bytes 811016 | tf_op jit(solution)/shard_map/ppermute | solution.py:105
  237.2 11.7 %copy-start.2 = (bf16[176,768]{1,0:T(8,128)(2,1)S(1)}, bf16[176,768]{1,0:T(8,128)(2,1)}, u32[]{:S(2)}) copy-start(bf16[176,768]{1,0:T(8,128)(2,1)} %copy-done.1) | copy-start | bytes 811012
  237.2 19.6 %copy-start.6 = (bf16[176,768]{1,0:T(8,128)(2,1)S(1)}, bf16[176,768]{1,0:T(8,128)(2,1)}, u32[]{:S(2)}) copy-start(bf16[176,768]{1,0:T(8,128)(2,1)} %copy-done.5) | copy-start | bytes 811012
  237.3 19.6 %copy-start.4 = (bf16[176,768]{1,0:T(8,128)(2,1)S(1)}, bf16[176,768]{1,0:T(8,128)(2,1)}, u32[]{:S(2)}) copy-start(bf16[176,768]{1,0:T(8,128)(2,1)} %copy-done.3) | copy-start | bytes 811012
  240.0 21.0 %copy-start.12 = (bf16[2,1408,128]{2,1,0:T(8,128)(2,1)S(1)}, bf16[2,1408,128]{2,1,0:T(8,128)(2,1)}, u32[]{:S(2)}) copy-start(bf16[2,1408,128]{2,1,0:T(8,128)(2,1)} %param.17) | copy-start | bytes 2162692
  240.0 12.9 %collective-permute-start.14 = (bf16[176,768]{1,0:T(8,128)(2,1)}, bf16[176,768]{1,0:T(8,128)(2,1)S(1)}, u32[]{:S(2)}, u32[]{:S(2)}) collective-permute-start(bf16[176,768]{1,0:T(8,128)(2,1)} %collective-permute-done.13), channel_id=1, source_target_pairs={{0,480},{32,0},{64,32},{96,64},{128,96},{160,128},{192,160},{224,1... | collective-permute-start | bytes 811016 | tf_op jit(solution)/shard_map/ppermute | solution.py:107
  263.4 40.3 %all-to-all-start.3 = ((bf16[2,32,24,128]{3,2,0,1:T(8,128)(2,1)}), bf16[2,32,24,128]{3,2,0,1:T(8,128)(2,1)S(1)}, u32[]{:S(2)}, u32[]{:S(2)}) async-start(bf16[2,32,24,128]{3,2,0,1:T(8,128)(2,1)} %pad_maximum_fusion), calls=%async_computation.3 | async-start | bytes 786432 | tf_op jit(solution)/shard_map/all_to_all | solution.py:125
  (3 other events, 18.8 us)
Sparse Core Ops, SparseCore 0:
  10.2 46.8 all-gather.2
  240.1 62.5 reduce-scatter.3
Sparse Core Ops, SparseCore 1:
  94.7 91.6 all-gather.4
